TPU v7x, 32 devices: a whole 2x2x4 slice. The times are simulated.
32 devices in a mesh: gx: 4 (over z), gy: 8 (over y, x, core).
Axes of the slice: x: 2, y: 2, z: 4, core: 2. Of those that a mesh axis runs over, the one named last changes fastest.
Arguments:
- radiance: bfloat16 [2048, 16, 128], P(('gx', 'gy')), may hold values from 0.049804688 to 2
- emission: float32 [2048, 16, 128], P(('gx', 'gy')), may hold values from 0.01 to 1
- reflectance: float32 [2048, 16, 128], P(('gx', 'gy')), may hold values from 0.1 to 0.9
- patch_area: float32 [2048, 128], P(('gx', 'gy')), may hold values from 0.25 to 4
- form_factor: bfloat16 [4096, 128, 128], P(('gx', 'gy')), may hold values from 0.00049972534 to 0.014953613
- source_index: int32 [32, 128], P(('gx', 'gy')), may hold values from 0 to 63
- target_index: int32 [32, 128], P(('gx', 'gy')), may hold values from 0 to 63
- block_index: int32 [32, 128], P(('gx', 'gy')), may hold values from 0 to 127, each once within a row
- valid_count: int32 [32, 32], P(('gx', 'gy')), may hold values from 0 to 4, as said below
Outputs:
- new_radiance: float32 [2048, 16, 128], P(('gx', 'gy'))
Inputs may be any that keep to these rules, and one draw needn't show every extreme that they name: `valid_count`: entry [d, p] is the number of live slots among the 4 slots of device d toward peer p, the live ones first; every row has an entry equal to 4. `block_index`: each row is a permutation of 0 to 127.
All inputs are finite; a program needn't handle non-finite values.
Results may differ from a plain program's by a relative error of at most 0.0012.
Values may be sent and summed in bfloat16 or wider, within the bound.
A program may use at most 128 MiB of HBM per device.

v0:
```python
import jax
import jax.numpy as jnp
from jax import lax
from jax.sharding import PartitionSpec as P


def shards(
    radiance,
    emission,
    reflectance,
    patch_area,
    form_factor,
    source_index,
    target_index,
    block_index,
    valid_count,
):
    peers = lax.axis_size(("gx", "gy"))
    clusters = radiance.shape[0]
    bands = radiance.shape[1]
    patches = radiance.shape[2]
    link_count = source_index.shape[1]
    slot_count = link_count // peers
    wanted_rows = source_index[0].reshape(peers, slot_count)
    asked_rows = lax.all_to_all(wanted_rows, ("gx", "gy"), split_axis=0, concat_axis=0, tiled=True)
    served = radiance[asked_rows]
    fetched = lax.all_to_all(served, ("gx", "gy"), split_axis=0, concat_axis=0, tiled=True)
    fetched = fetched.reshape(link_count, bands, patches)
    position = jnp.arange(link_count, dtype=jnp.int32)
    block_row = block_index[0]
    stored_link = jnp.zeros((link_count,), jnp.int32).at[block_row].set(position)
    live_count = valid_count[0]
    live_link = (position % slot_count < live_count[position // slot_count]).astype(jnp.float32)
    live_stored = live_link[stored_link]
    target_stored = target_index[0][stored_link]
    rad_stored = fetched[stored_link]
    forward = jnp.einsum(
        "mij,mbj->mbi", form_factor, rad_stored, preferred_element_type=jnp.float32
    )
    cluster_ids = jnp.arange(clusters, dtype=jnp.int32)
    target_table = (cluster_ids[:, None] == target_stored[None, :]).astype(
        jnp.float32
    ) * live_stored[None, :]
    gathered = jnp.dot(
        target_table,
        forward.reshape(link_count, bands * patches),
        precision=lax.Precision.HIGHEST,
        preferred_element_type=jnp.float32,
    )
    weighted = (patch_area[:, None, :] * radiance.astype(jnp.float32)).astype(jnp.bfloat16)
    weighted_stored = weighted[target_stored]
    backward = jnp.einsum(
        "mij,mbi->mbj", form_factor, weighted_stored, preferred_element_type=jnp.float32
    )
    backward = (backward * live_stored[:, None, None]).astype(jnp.bfloat16)
    backward_links = backward[block_row]
    arrived = lax.all_to_all(
        backward_links.reshape(peers, slot_count, bands, patches),
        ("gx", "gy"),
        split_axis=0,
        concat_axis=0,
        tiled=True,
    )
    arrived = arrived.reshape(link_count, bands * patches).astype(jnp.float32)
    source_table = (cluster_ids[:, None] == asked_rows.reshape(link_count)[None, :]).astype(
        jnp.float32
    )
    returned = jnp.dot(
        source_table, arrived, precision=lax.Precision.HIGHEST, preferred_element_type=jnp.float32
    )
    irradiance = (
        gathered.reshape(clusters, bands, patches)
        + returned.reshape(clusters, bands, patches) / patch_area[:, None, :]
    )
    return emission + reflectance * irradiance


def solution(mesh):
    in_specs = (
        P(("gx", "gy"), None, None),
        P(("gx", "gy"), None, None),
        P(("gx", "gy"), None, None),
        P(("gx", "gy"), None),
        P(("gx", "gy"), None, None),
        P(("gx", "gy"), None),
        P(("gx", "gy"), None),
        P(("gx", "gy"), None),
        P(("gx", "gy"), None),
    )
    out_specs = P(("gx", "gy"), None, None)
    return jax.shard_map(shards, mesh=mesh, in_specs=in_specs, out_specs=out_specs, check_vma=False)
```

profile of v0, /device:TPU:0, one launch (start us, length us, event | category | flops | bytes accessed | tf_op | source)
XLA Modules:
  0.0 72.1 jit_solution(4436506217157670074)
XLA Ops:
  0.0 0.5 broadcast.170
  0.5 1.2 %reduce.6 = s32[128]{0:T(128)S(1)} reduce(s32[1,128]{1,0:T(1,128)} %param.14, s32[]{:T(128)} %broadcast.170), dimensions={0}, to_apply=%param.14.reduce_sub_computation.3 | reduce | bytes 1028 | tf_op args[5]
  1.7 0.7 all_to_all.14
  2.4 7.3 %all-to-all-start = ((s32[32,1,4]{2,1,0:T(1,128)}), s32[32,1,4]{2,1,0:T(1,128)S(1)}, u32[]{:S(2)}, u32[]{:S(2)}) async-start(s32[32,1,4]{2,1,0:T(1,128)} %bitcast.6), calls=%async_computation | async-start | bytes 32768 | tf_op jit(solution)/shard_map/all_to_all | solution.py:25
  9.8 0.7 fusion.12
  10.5 1.0 %scatter_custom_fusion = s32[128]{0:T(128)S(1)} fusion(s32[128]{0:T(128)S(1)} %fusion.12, s32[128]{0:T(128)S(1)} %iota.12, s32[]{:T(128)} %constant.32.clone.1), kind=kCustom, calls=%fused_computation.45 | custom fusion | bytes 516 | tf_op jit(solution)/shard_map/scatter | solution.py:31
  11.5 1.2 %gather_fusion = s32[128]{0:T(128)S(1)} fusion(s32[128]{0:T(128)S(1)} %bitcast.49, s32[1024]{0:T(1024)S(1)} %pad_clamp_fusion.4), kind=kCustom, calls=%fused_computation | custom fusion | bytes 1536 | tf_op jit(solution)/shard_map/gather | solution.py:35
  12.7 1.6 %gather_fusion.1 = s32[128]{0:T(128)S(1)} fusion(s32[32]{0:T(128)} %bitcast.50, s32[1024]{0:T(1024)S(1)} %pad_clamp_fusion.3), kind=kCustom, calls=%fused_computation.1 | custom fusion | bytes 1536 | tf_op jit(solution)/shard_map/gather | solution.py:33
  14.3 1.2 %gather_fusion.2 = f32[128]{0:T(128)S(1)} fusion(f32[128]{0:T(128)S(1)} %compare_convert_fusion, s32[1024]{0:T(1024)S(1)} %pad_clamp_fusion.4), kind=kCustom, calls=%fused_computation.2 | custom fusion | bytes 1536 | tf_op jit(solution)/shard_map/gather | solution.py:34
  15.6 1.0 %multiply_convert_fusion = bf16[64,16,128]{2,0,1:T(8,128)(2,1)S(1)} fusion(bf16[64,16,128]{2,1,0:T(8,128)(2,1)} %param.9, f32[64,128]{1,0:T(8,128)} %param.12), kind=kLoop, calls=%fused_computation.16 | loop fusion | flops 393216 | bytes 557056 | tf_op jit(solution)/shard_map/convert_element_type | solution.py:50
  16.8 0.7 gather_fusion.5
  17.5 3.4 %fusion = bf16[128,16,128]{2,1,0:T(8,128)(2,1)S(1)} fusion(bf16[128,16,128]{2,1,0:T(8,128)(2,1)S(1)} %gather_fusion.5, bf16[128,128,128]{2,1,0:T(8,128)(2,1)} %param.13, f32[128]{0:T(128)S(1)} %gather_fusion.2), kind=kOutput, calls=%fused_computation.9 | convolution fusion | flops 67633152 | bytes 5243392 | tf_op jit(solution)/shard_map/mij,mbi->mbj/dot_general | solution.py:52
  20.9 1.5 %gather_fusion.6 = bf16[128,16,128]{2,1,0:T(8,128)(2,1)} fusion(bf16[128,16,128]{2,1,0:T(8,128)(2,1)S(1)} %fusion, s32[1024]{0:T(1024)S(1)} %pad_clamp_fusion), kind=kCustom, calls=%fused_computation.6 | custom fusion | bytes 1049088 | tf_op jit(solution)/shard_map/gather | solution.py:56
  22.4 5.8 %all-to-all-start.2 = ((bf16[32,4,16,128]{3,2,1,0:T(8,128)(2,1)}), bf16[32,4,16,128]{3,2,1,0:T(8,128)(2,1)S(1)}, u32[]{:S(2)}, u32[]{:S(2)}) async-start(bf16[32,4,16,128]{3,2,1,0:T(8,128)(2,1)} %bitcast.15), calls=%async_computation.2 | async-start | bytes 1048576 | tf_op jit(solution)/shard_map/all_to_all | solution.py:57
  28.6 1.5 %gather_fusion.3 = bf16[128,16,128]{2,1,0:T(8,128)(2,1)} fusion(bf16[64,16,128]{2,1,0:T(8,128)(2,1)S(1)} %copy-done.1, s32[1024]{0:T(1024)S(1)} %pad_clamp_fusion.2), kind=kCustom, calls=%fused_computation.3 | custom fusion | bytes 1049088 | tf_op jit(solution)/shard_map/gather | solution.py:26
  30.1 13.8 %all-to-all-done.2 = bf16[32,4,16,128]{3,2,1,0:T(8,128)(2,1)S(1)} async-done(((bf16[32,4,16,128]{3,2,1,0:T(8,128)(2,1)}), bf16[32,4,16,128]{3,2,1,0:T(8,128)(2,1)S(1)}, u32[]{:S(2)}, u32[]{:S(2)}) %all-to-all-start.2) | async-done | bytes 524320 | tf_op jit(solution)/shard_map/all_to_all | solution.py:57
  43.9 3.0 %all-to-all-start.1 = ((bf16[32,4,16,128]{3,2,1,0:T(8,128)(2,1)}), bf16[32,4,16,128]{3,2,1,0:T(8,128)(2,1)S(1)}, u32[]{:S(2)}, u32[]{:S(2)}) async-start(bf16[32,4,16,128]{3,2,1,0:T(8,128)(2,1)} %bitcast.8), calls=%async_computation.1 | async-start | bytes 1048576 | tf_op jit(solution)/shard_map/all_to_all | solution.py:27
  46.9 0.6 reduce.7
  48.0 1.1 %convolution_divide_fusion = f32[64,16,128]{2,0,1:T(8,128)} fusion(bf16[16,128,128]{2,1,0:T(8,128)(2,1)S(1)} %bitcast.57, f32[64,128]{1,0:T(8,128)S(1)} %copy-done.4, s32[128]{0:T(128)S(1)} %eq.34), kind=kOutput, calls=%fused_computation.13 | convolution fusion | flops 33693696 | bytes 1081856 | tf_op jit(solution)/shard_map/dot_general | solution.py:68
  49.1 13.4 %all-to-all-done.1 = bf16[32,4,16,128]{3,2,1,0:T(8,128)(2,1)S(1)} async-done(((bf16[32,4,16,128]{3,2,1,0:T(8,128)(2,1)}), bf16[32,4,16,128]{3,2,1,0:T(8,128)(2,1)S(1)}, u32[]{:S(2)}, u32[]{:S(2)}) %all-to-all-start.1) | async-done | bytes 524320 | tf_op jit(solution)/shard_map/all_to_all | solution.py:27
  62.5 0.7 gather_fusion.4
  63.2 4.5 %fusion.17 = f32[128,16,128]{2,1,0:T(8,128)S(1)} fusion(bf16[128,16,128]{2,1,0:T(8,128)(2,1)S(1)} %gather_fusion.4, bf16[128,128,128]{2,1,0:T(8,128)(2,1)} %param.13), kind=kOutput, calls=%fused_computation.48 | convolution fusion | flops 67108864 | bytes 5767168 | tf_op jit(solution)/shard_map/mij,mbj->mbi/dot_general | solution.py:37
  68.5 2.6 %fusion.2 = f32[64,16,128]{2,0,1:T(8,128)S(1)} fusion(f32[64,16,128]{2,0,1:T(8,128)} %convolution_divide_fusion, f32[16,128,128]{2,1,0:T(8,128)S(1)} %bitcast.51, f32[64,16,128]{2,1,0:T(8,128)S(1)} %copy-done.2, f32[64,16,128]{2,1,0:T(8,128)S(1)} %copy-done.3, f32[128]{0:T(128)S(1)} %gather_fusion.2, s32[128]{0:T(128)S(1)} %gather_fusion), kind=kOutput, calls=%fused_computation.12 | convolution fusion | flops 201736192 | bytes 3146752 | tf_op jit(solution)/shard_map/dot_general | solution.py:44
  71.0 1.1 %copy.37 = f32[64,16,128]{2,1,0:T(8,128)} copy(f32[64,16,128]{2,0,1:T(8,128)S(1)} %fusion.2) | data formatting | bytes 1048576 | tf_op jit(solution)/shard_map/add | solution.py:75
  (31 shorter events, 1.8 us)
Async XLA Ops:
  0.0 11.5 %copy-start = (s32[1,128]{1,0:T(1,128)S(1)}, s32[1,128]{1,0:T(1,128)}, u32[]{:S(2)}) copy-start(s32[1,128]{1,0:T(1,128)} %param.15) | copy-start | bytes 1540
  2.4 20.0 %all-to-all-start = ((s32[32,1,4]{2,1,0:T(1,128)}), s32[32,1,4]{2,1,0:T(1,128)S(1)}, u32[]{:S(2)}, u32[]{:S(2)}) async-start(s32[32,1,4]{2,1,0:T(1,128)} %bitcast.6), calls=%async_computation | async-start | bytes 32768 | tf_op jit(solution)/shard_map/all_to_all | solution.py:25
  16.8 11.8 %copy-start.1 = (bf16[64,16,128]{2,1,0:T(8,128)(2,1)S(1)}, bf16[64,16,128]{2,1,0:T(8,128)(2,1)}, u32[]{:S(2)}) copy-start(bf16[64,16,128]{2,1,0:T(8,128)(2,1)} %param.9) | copy-start | bytes 786436
  20.9 27.1 %copy-start.4 = (f32[64,128]{1,0:T(8,128)S(1)}, f32[64,128]{1,0:T(8,128)}, u32[]{:S(2)}) copy-start(f32[64,128]{1,0:T(8,128)} %param.12) | copy-start | bytes 98308
  22.4 21.5 %all-to-all-start.2 = ((bf16[32,4,16,128]{3,2,1,0:T(8,128)(2,1)}), bf16[32,4,16,128]{3,2,1,0:T(8,128)(2,1)S(1)}, u32[]{:S(2)}, u32[]{:S(2)}) async-start(bf16[32,4,16,128]{3,2,1,0:T(8,128)(2,1)} %bitcast.15), calls=%async_computation.2 | async-start | bytes 1048576 | tf_op jit(solution)/shard_map/all_to_all | solution.py:57
  43.9 18.6 %all-to-all-start.1 = ((bf16[32,4,16,128]{3,2,1,0:T(8,128)(2,1)}), bf16[32,4,16,128]{3,2,1,0:T(8,128)(2,1)S(1)}, u32[]{:S(2)}, u32[]{:S(2)}) async-start(bf16[32,4,16,128]{3,2,1,0:T(8,128)(2,1)} %bitcast.8), calls=%async_computation.1 | async-start | bytes 1048576 | tf_op jit(solution)/shard_map/all_to_all | solution.py:27
  63.2 5.3 %copy-start.2 = (f32[64,16,128]{2,1,0:T(8,128)S(1)}, f32[64,16,128]{2,1,0:T(8,128)}, u32[]{:S(2)}) copy-start(f32[64,16,128]{2,1,0:T(8,128)} %param.10) | copy-start | bytes 1572868
  63.2 5.3 %copy-start.3 = (f32[64,16,128]{2,1,0:T(8,128)S(1)}, f32[64,16,128]{2,1,0:T(8,128)}, u32[]{:S(2)}) copy-start(f32[64,16,128]{2,1,0:T(8,128)} %param.11) | copy-start | bytes 1572868
where the time goes:
time: 72.6 us; the launch traced here: 72.1 us
  waiting for transfers between devices  27.2 us (37%)
  starting transfers between devices  16.1 us (22%)
  local copies, waits for them, and re-layouts  13.4 us (18%)
  matrix products  11.6 us (16%)
  other arithmetic  3.58 us (5%)
    all_to_all x1, waiting for transfers between devices, shards(): lax.all_to_all(backward_links.reshape(peers, slot_count, bands, patches),...  13.8 us
    all_to_all x1, waiting for transfers between devices, shards(): lax.all_to_all(served, ('gx', 'gy'), split_axis=0, concat_axis=0, tiled=T...  13.4 us
    all_to_all x1, starting transfers between devices, shards(): lax.all_to_all(wanted_rows, ('gx', 'gy'), split_axis=0, concat_axis=0, ti...  7.33 us
    all_to_all x1, starting transfers between devices, shards(): lax.all_to_all(backward_links.reshape(peers, slot_count, bands, patches),...  5.84 us
    dot_general x1, matrix products, shards(): jnp.einsum('mij,mbj->mbi', form_factor, rad_stored, preferred_element_typ...  4.54 us
    dot_general x1, matrix products, shards(): jnp.einsum('mij,mbi->mbj', form_factor, weighted_stored, preferred_elemen...  3.39 us
    all_to_all x1, starting transfers between devices, shards(): lax.all_to_all(served, ('gx', 'gy'), split_axis=0, concat_axis=0, tiled=T...  2.97 us
    dot_general x1, matrix products, shards(): jnp.dot(target_table, forward.reshape(link_count, bands * patches), preci...  2.56 us
  transfers between devices with their start and end apart: 3, of which 2 were waited for; matrix products, arithmetic and copies ran while one was open for 23% of the time, Pallas kernels for 0%

commit v1 on v0

v1 whole, which is shorter than its diff:
```python
import functools

import jax
import jax.numpy as jnp
from jax import lax
from jax.experimental import pallas as pl
from jax.experimental.pallas import tpu as pltpu
from jax.sharding import PartitionSpec as P

MESH = pl.DeviceIdType.MESH
GROUP = 4
LANES = 128
F32 = jnp.float32
BF16 = jnp.bfloat16


def exchange(
    n,
    inner,
    block_ref,
    target_ref,
    count_ref,
    source_ref,
    rad_ref,
    area_ref,
    form_hbm,
    fwd_ref,
    arrived_ref,
    asked_out,
    form_ref,
    weighted_ref,
    bwd_ref,
    served_ref,
    fetched_ref,
    asked_vmem,
    asked_ref,
    form_sem,
    asked_sem,
    send_sems,
    idx_sem,
    bwd_sem,
    rad_sem,
):
    me = lax.axis_index("gx") * inner + lax.axis_index("gy")
    links = block_ref.shape[1]
    slots = links // n
    clusters = rad_ref.shape[0]
    parts = form_sem.shape[0]
    step = links // parts

    def coords(p):
        return (p // inner, p % inner)

    def form_copy(i):
        rows = pl.ds(i * step, step)
        return pltpu.make_async_copy(form_hbm.at[rows], form_ref.at[rows], form_sem.at[i])

    for i in range(parts):
        form_copy(i).start()

    barrier = pltpu.get_barrier_semaphore()

    def greet(k, c):
        pl.semaphore_signal(
            barrier, inc=1, device_id=coords((me + k) % n), device_id_type=MESH
        )
        return c

    lax.fori_loop(1, n, greet, 0)

    def weigh(c, carry):
        area = area_ref[pl.ds(c, 1), :]
        weighted_ref[c] = (area * rad_ref[c].astype(F32)).astype(BF16)
        return carry

    lax.fori_loop(0, clusters, weigh, 0, unroll=8)

    pl.semaphore_wait(barrier, n - 1)

    width = asked_vmem.shape[2]

    def lane_base(p):
        if links == width:
            return 0
        return pl.multiple_of(p * slots // width * width, width)

    def idx_copy(k):
        p = (me + k) % n
        return pltpu.make_async_remote_copy(
            src_ref=source_ref.at[:, pl.ds(lane_base(p), width)],
            dst_ref=asked_vmem.at[me],
            send_sem=send_sems.at[0],
            recv_sem=idx_sem.at[k],
            device_id=coords(p),
            device_id_type=MESH,
        )

    def send_idx(k, c):
        idx_copy(k).start()
        return c

    lax.fori_loop(1, n, send_idx, 0)
    asked_vmem[me] = source_ref[:, pl.ds(lane_base(me), width)]

    def bwd_copy(k):
        p = (me + k) % n
        return pltpu.make_async_remote_copy(
            src_ref=bwd_ref.at[pl.ds(p * slots, slots)],
            dst_ref=arrived_ref.at[pl.ds(me * slots, slots)],
            send_sem=send_sems.at[1],
            recv_sem=bwd_sem.at[k],
            device_id=coords(p),
            device_id_type=MESH,
        )

    def rad_copy(k):
        p = (me + k) % n
        return pltpu.make_async_remote_copy(
            src_ref=served_ref.at[pl.ds(p * slots, slots)],
            dst_ref=fetched_ref.at[pl.ds(me * slots, slots)],
            send_sem=send_sems.at[2],
            recv_sem=rad_sem.at[k],
            device_id=coords(p),
            device_id_type=MESH,
        )

    def live_of(p, s):
        return jnp.where(s < count_ref[0, p], 1.0, 0.0).astype(F32)

    for i in range(parts):
        form_copy(i).wait()

    def backward(t, c):
        for u in range(GROUP):
            p = (me + t * GROUP + u) % n
            for s in range(slots):
                l = p * slots + s
                form = form_ref[block_ref[0, l]]
                seen = weighted_ref[target_ref[0, l]]
                got = jnp.dot(seen, form, preferred_element_type=F32)
                bwd_ref[l] = (got * live_of(p, s)).astype(BF16)
        for u in range(GROUP):
            k = t * GROUP + u

            @pl.when(k != 0)
            def _():
                bwd_copy(k).start()

        return c

    lax.fori_loop(0, n // GROUP, backward, 0)

    def wait_idx(k, c):
        idx_copy(k).wait_recv()
        return c

    lax.fori_loop(1, n, wait_idx, 0)
    to_smem = pltpu.make_async_copy(asked_vmem, asked_ref, asked_sem)
    to_smem.start()
    to_smem.wait()
    base = me * slots % width

    def serve(k, c):
        p = (me + k) % n
        for s in range(slots):
            served_ref[p * slots + s] = rad_ref[asked_ref[p, 0, base + s]]
            asked_out[0, p * slots + s] = asked_ref[p, 0, base + s]

        @pl.when(k != 0)
        def _():
            rad_copy(k).start()

        return c

    lax.fori_loop(0, n, serve, 0)
    own = pl.ds(me * slots, slots)
    fetched_ref[own] = served_ref[own]
    arrived_ref[own] = bwd_ref[own]

    def forward(t, c):
        for u in range(GROUP):
            k = t * GROUP + u

            @pl.when(k != 0)
            def _():
                rad_copy(k).wait_recv()

        for u in range(GROUP):
            p = (me + n - t * GROUP - u) % n
            for s in range(slots):
                l = p * slots + s
                form = form_ref[block_ref[0, l]]
                got = lax.dot_general(
                    fetched_ref[l], form, (((1,), (1,)), ((), ())), preferred_element_type=F32
                )
                fwd_ref[l] = got * live_of(p, s)
        return c

    lax.fori_loop(0, n // GROUP, forward, 0)

    def wait_bwd(k, c):
        bwd_copy(k).wait_recv()
        return c

    lax.fori_loop(1, n, wait_bwd, 0)
    most = pl.ds(0, (n - 1) * slots)
    for buf, which in ((bwd_ref, 1), (served_ref, 2)):
        pltpu.make_async_copy(buf.at[most], buf.at[most], send_sems.at[which]).wait()
    rows = asked_vmem.at[pl.ds(0, n - 1)]
    pltpu.make_async_copy(rows, rows, send_sems.at[0]).wait()


def combine(
    target_ref, asked_ref, fwd_ref, arrived_ref, em_ref, refl_ref, area_ref, out_ref, gath, ret
):
    clusters = em_ref.shape[0]
    links = fwd_ref.shape[0]

    def clear(c, carry):
        gath[c] = jnp.zeros(gath.shape[1:], F32)
        ret[c] = jnp.zeros(ret.shape[1:], F32)
        return carry

    lax.fori_loop(0, clusters, clear, 0, unroll=8)

    def scatter(l, carry):
        t = target_ref[0, l]
        s = asked_ref[0, l]
        gath[t] += fwd_ref[l]
        ret[s] += arrived_ref[l].astype(F32)
        return carry

    lax.fori_loop(0, links, scatter, 0, unroll=8)

    def finish(c, carry):
        area = area_ref[pl.ds(c, 1), :]
        out_ref[c] = em_ref[c] + refl_ref[c] * (gath[c] + ret[c] / area)
        return carry

    lax.fori_loop(0, clusters, finish, 0, unroll=8)


def solution(mesh):
    outer, inner = mesh.shape["gx"], mesh.shape["gy"]
    n = outer * inner

    def shards(
        radiance,
        emission,
        reflectance,
        patch_area,
        form_factor,
        source_index,
        target_index,
        block_index,
        valid_count,
    ):
        clusters, bands, patches = radiance.shape
        links = source_index.shape[1]
        slots = links // n
        tile = (bands, patches)
        vm = pl.BlockSpec(memory_space=pltpu.VMEM)
        sm = pl.BlockSpec(memory_space=pltpu.SMEM)
        hbm = pl.BlockSpec(memory_space=pl.ANY)
        width = min(links, LANES)
        parts = 4
        fwd, arrived, asked = pl.pallas_call(
            functools.partial(exchange, n, inner),
            out_shape=(
                jax.ShapeDtypeStruct((links,) + tile, F32),
                jax.ShapeDtypeStruct((links,) + tile, BF16),
                jax.ShapeDtypeStruct((1, links), jnp.int32),
            ),
            in_specs=[sm, sm, sm, vm, vm, vm, hbm],
            out_specs=(vm, vm, sm),
            scratch_shapes=[
                pltpu.VMEM(form_factor.shape, BF16),
                pltpu.VMEM((clusters,) + tile, BF16),
                pltpu.VMEM((links,) + tile, BF16),
                pltpu.VMEM((links,) + tile, BF16),
                pltpu.VMEM((links,) + tile, BF16),
                pltpu.VMEM((n, 1, width), jnp.int32),
                pltpu.SMEM((n, 1, width), jnp.int32),
                pltpu.SemaphoreType.DMA((parts,)),
                pltpu.SemaphoreType.DMA,
                pltpu.SemaphoreType.DMA((3,)),
                pltpu.SemaphoreType.DMA((n,)),
                pltpu.SemaphoreType.DMA((n,)),
                pltpu.SemaphoreType.DMA((n,)),
            ],
            compiler_params=pltpu.CompilerParams(
                collective_id=0, has_side_effects=True, vmem_limit_bytes=60 * 1024 * 1024
            ),
            name="exchange",
        )(
            block_index,
            target_index,
            valid_count,
            source_index,
            radiance,
            patch_area,
            form_factor,
        )
        return pl.pallas_call(
            combine,
            out_shape=jax.ShapeDtypeStruct((clusters,) + tile, F32),
            in_specs=[sm, sm, vm, vm, vm, vm, vm],
            out_specs=vm,
            scratch_shapes=[pltpu.VMEM((clusters,) + tile, F32)] * 2,
            compiler_params=pltpu.CompilerParams(vmem_limit_bytes=24 * 1024 * 1024),
            name="combine",
        )(target_index, asked, fwd, arrived, emission, reflectance, patch_area)

    spec3 = P(("gx", "gy"), None, None)
    spec2 = P(("gx", "gy"), None)
    return jax.shard_map(
        shards,
        mesh=mesh,
        in_specs=(spec3, spec3, spec3, spec2, spec3, spec2, spec2, spec2, spec2),
        out_specs=spec3,
        check_vma=False,
    )
```

time: 72.6 us -> 39.5 us (0.54)
  the two profiles are of different devices: /device:TPU:0 before, /device:TPU:29 now
where the time goes in v1:
time: 39.5 us; the launch traced here: 39.2 us
  Pallas kernels  36.3 us (92%)
  local copies, waits for them, and re-layouts  2.9 us (7%)
    pallas_call x1, Pallas kernels, shards(): pl.pallas_call(functools.partial(exchange, n, inner), out_shape=(jax.Shap...  34.1 us
    unnamed x14, local copies, waits for them, and re-layouts  2.9 us
    pallas_call x1, Pallas kernels, shards(): pl.pallas_call(combine, out_shape=jax.ShapeDtypeStruct((clusters,) + tile...  2.16 us

profile of v1, /device:TPU:29, one launch (start us, length us, event | category | flops | bytes accessed | tf_op | source)
XLA Modules:
  0.0 39.2 jit_solution(9841544667204545754)
XLA Ops:
  0.0 0.0 copy-start.5
  0.0 0.0 copy-start.4
  0.0 0.0 copy-start.2
  0.0 0.0 copy-start.1
  0.0 34.1 %exchange.1 = (f32[128,16,128]{2,1,0:T(8,128)}, bf16[128,16,128]{2,1,0:T(8,128)(2,1)}, s32[1,128]{1,0:T(1,128)}) custom-call(s32[1,128]{1,0:T(1,128)} %block_ref.1, s32[1,128]{1,0:T(1,128)} %target_ref.3, s32[1,32]{1,0:T(1,128)} %count_ref.1, s32[1,128]{1,0:T(1,128)} %source_ref.1, bf16[64,16,128]{2,1,0:T(8,128)(2,1)} %rad_ref.1, f32[64,128]{1,0:T(8,128)} %area_ref.3, ...), custom_call_target="tpu_custom_call" | custom-call | tf_op jit(solution)/shard_map/exchange/pallas_call | solution.py:267
  34.1 0.0 copy-done.5
  34.2 0.0 copy-done.4
  34.2 0.0 copy-done.2
  34.2 0.0 copy-done.1
  34.2 0.0 copy-start
  34.2 1.2 %copy-done = f32[128,16,128]{2,1,0:T(8,128)S(1)} copy-done((f32[128,16,128]{2,1,0:T(8,128)S(1)}, f32[128,16,128]{2,1,0:T(8,128)}, u32[]{:S(2)}) %copy-start) | copy-done | bytes 1048600
  35.4 0.0 copy-start.3
  35.4 1.0 %copy-done.3 = bf16[128,16,128]{2,1,0:T(8,128)(2,1)S(1)} copy-done((bf16[128,16,128]{2,1,0:T(8,128)(2,1)S(1)}, bf16[128,16,128]{2,1,0:T(8,128)(2,1)}, u32[]{:S(2)}) %copy-start.3) | copy-done | bytes 524312
  36.5 0.0 copy-start.6
  36.5 0.6 %copy-done.6 = s32[1,128]{1,0:T(1,128)S(1)} copy-done((s32[1,128]{1,0:T(1,128)S(1)}, s32[1,128]{1,0:T(1,128)}, u32[]{:S(2)}) %copy-start.6) | copy-done | bytes 536
  37.1 2.2 %combine.1 = f32[64,16,128]{2,1,0:T(8,128)} custom-call(s32[1,128]{1,0:T(1,128)S(1)} %copy-done.5, s32[1,128]{1,0:T(1,128)S(1)} %copy-done.6, f32[128,16,128]{2,1,0:T(8,128)S(1)} %copy-done, bf16[128,16,128]{2,1,0:T(8,128)(2,1)S(1)} %copy-done.3, f32[64,16,128]{2,1,0:T(8,128)S(1)} %copy-done.1, f32[64,16,128]{2,1,0:T(8,128)S(1)} %copy-done.2, ...), custom_call_target="tpu_custom_call" | custom-call | tf_op jit(solution)/shard_map/combine/pallas_call | solution.py:304
Async XLA Ops:
  0.0 34.1 %copy-start.5 = (s32[1,128]{1,0:T(1,128)S(1)}, s32[1,128]{1,0:T(1,128)}, u32[]{:S(2)}) copy-start(s32[1,128]{1,0:T(1,128)} %target_ref.3) | copy-start | bytes 1540
  0.0 34.2 %copy-start.4 = (f32[64,128]{1,0:T(8,128)S(1)}, f32[64,128]{1,0:T(8,128)}, u32[]{:S(2)}) copy-start(f32[64,128]{1,0:T(8,128)} %area_ref.3) | copy-start | bytes 98308
  0.0 34.2 %copy-start.2 = (f32[64,16,128]{2,1,0:T(8,128)S(1)}, f32[64,16,128]{2,1,0:T(8,128)}, u32[]{:S(2)}) copy-start(f32[64,16,128]{2,1,0:T(8,128)} %refl_ref.1) | copy-start | bytes 1572868
  0.0 34.2 %copy-start.1 = (f32[64,16,128]{2,1,0:T(8,128)S(1)}, f32[64,16,128]{2,1,0:T(8,128)}, u32[]{:S(2)}) copy-start(f32[64,16,128]{2,1,0:T(8,128)} %em_ref.1) | copy-start | bytes 1572868
  34.2 1.2 %copy-start = (f32[128,16,128]{2,1,0:T(8,128)S(1)}, f32[128,16,128]{2,1,0:T(8,128)}, u32[]{:S(2)}) copy-start(f32[128,16,128]{2,1,0:T(8,128)} %get-tuple-element.9.fwd_ref) | copy-start | bytes 3145732
  35.4 1.0 %copy-start.3 = (bf16[128,16,128]{2,1,0:T(8,128)(2,1)S(1)}, bf16[128,16,128]{2,1,0:T(8,128)(2,1)}, u32[]{:S(2)}) copy-start(bf16[128,16,128]{2,1,0:T(8,128)(2,1)} %get-tuple-element.10.arrived_ref) | copy-start | bytes 1572868
  36.5 0.6 %copy-start.6 = (s32[1,128]{1,0:T(1,128)S(1)}, s32[1,128]{1,0:T(1,128)}, u32[]{:S(2)}) copy-start(s32[1,128]{1,0:T(1,128)} %get-tuple-element.8.asked_ref) | copy-start | bytes 1540

commit v2 on v1

--- a/solution.py
+++ b/solution.py
@@ -10,6 +10,8 @@
 MESH = pl.DeviceIdType.MESH
 GROUP = 4
 LANES = 128
+EXCHANGE_MIB = 60
+COMBINE_MIB = 60
 F32 = jnp.float32
 BF16 = jnp.bfloat16
 
@@ -17,25 +19,33 @@
 def exchange(
     n,
     inner,
+    block_hbm,
+    target_hbm,
+    count_hbm,
+    source_hbm,
+    rad_hbm,
+    area_hbm,
+    form_hbm,
+    fwd_hbm,
+    arrived_hbm,
+    asked_hbm,
     block_ref,
     target_ref,
     count_ref,
     source_ref,
     rad_ref,
     area_ref,
-    form_hbm,
-    fwd_ref,
-    arrived_ref,
-    asked_out,
     form_ref,
     weighted_ref,
     bwd_ref,
     served_ref,
     fetched_ref,
+    fwd_ref,
     asked_vmem,
     asked_ref,
     form_sem,
-    asked_sem,
+    in_sem,
+    out_sem,
     send_sems,
     idx_sem,
     bwd_sem,
@@ -51,12 +61,27 @@
     def coords(p):
         return (p // inner, p % inner)
 
-    def form_copy(i):
-        rows = pl.ds(i * step, step)
-        return pltpu.make_async_copy(form_hbm.at[rows], form_ref.at[rows], form_sem.at[i])
-
-    for i in range(parts):
-        form_copy(i).start()
+    loads = [
+        pltpu.make_async_copy(src, dst, in_sem.at[i])
+        for i, (src, dst) in enumerate(
+            (
+                (rad_hbm, rad_ref),
+                (area_hbm, area_ref),
+                (block_hbm, block_ref),
+                (target_hbm, target_ref),
+                (count_hbm, count_ref),
+                (source_hbm, source_ref),
+            )
+        )
+    ]
+    forms = [
+        pltpu.make_async_copy(
+            form_hbm.at[pl.ds(i * step, step)], form_ref.at[pl.ds(i * step, step)], form_sem.at[i]
+        )
+        for i in range(parts)
+    ]
+    for load in loads + forms:
+        load.start()
 
     barrier = pltpu.get_barrier_semaphore()
 
@@ -67,6 +92,9 @@
         return c
 
     lax.fori_loop(1, n, greet, 0)
+
+    for load in loads:
+        load.wait()
 
     def weigh(c, carry):
         area = area_ref[pl.ds(c, 1), :]
@@ -74,8 +102,6 @@
         return carry
 
     lax.fori_loop(0, clusters, weigh, 0, unroll=8)
-
-    pl.semaphore_wait(barrier, n - 1)
 
     width = asked_vmem.shape[2]
 
@@ -95,18 +121,11 @@
             device_id_type=MESH,
         )
 
-    def send_idx(k, c):
-        idx_copy(k).start()
-        return c
-
-    lax.fori_loop(1, n, send_idx, 0)
-    asked_vmem[me] = source_ref[:, pl.ds(lane_base(me), width)]
-
     def bwd_copy(k):
         p = (me + k) % n
         return pltpu.make_async_remote_copy(
             src_ref=bwd_ref.at[pl.ds(p * slots, slots)],
-            dst_ref=arrived_ref.at[pl.ds(me * slots, slots)],
+            dst_ref=arrived_hbm.at[pl.ds(me * slots, slots)],
             send_sem=send_sems.at[1],
             recv_sem=bwd_sem.at[k],
             device_id=coords(p),
@@ -127,35 +146,61 @@
     def live_of(p, s):
         return jnp.where(s < count_ref[0, p], 1.0, 0.0).astype(F32)
 
-    for i in range(parts):
-        form_copy(i).wait()
-
-    def backward(t, c):
+    for form in forms:
+        form.wait()
+
+    def back(t):
         for u in range(GROUP):
-            p = (me + t * GROUP + u) % n
+            p = (me + 1 + t * GROUP + u) % n
             for s in range(slots):
                 l = p * slots + s
                 form = form_ref[block_ref[0, l]]
                 seen = weighted_ref[target_ref[0, l]]
                 got = jnp.dot(seen, form, preferred_element_type=F32)
                 bwd_ref[l] = (got * live_of(p, s)).astype(BF16)
+
+    def back_only(t, c):
+        back(t)
+        return c
+
+    def send_bwd(k, c):
+        bwd_copy(k).start()
+        return c
+
+    def back_send(t, c):
+        back(t)
         for u in range(GROUP):
-            k = t * GROUP + u
-
-            @pl.when(k != 0)
+            k = 1 + t * GROUP + u
+
+            @pl.when(k != n)
             def _():
                 bwd_copy(k).start()
 
         return c
 
-    lax.fori_loop(0, n // GROUP, backward, 0)
+    early = n // GROUP // 2
+    lax.fori_loop(0, early, back_only, 0)
+    pl.semaphore_wait(barrier, n - 1)
+
+    def send_idx(k, c):
+        idx_copy(k).start()
+        return c
+
+    lax.fori_loop(1, n, send_idx, 0)
+    lax.fori_loop(1, 1 + early * GROUP, send_bwd, 0)
+    asked_vmem[me] = source_ref[:, pl.ds(lane_base(me), width)]
+    lax.fori_loop(early, n // GROUP, back_send, 0)
+
+    own = pl.ds(me * slots, slots)
+    keep_own = pltpu.make_async_copy(bwd_ref.at[own], arrived_hbm.at[own], out_sem.at[0])
+    keep_own.start()
 
     def wait_idx(k, c):
         idx_copy(k).wait_recv()
         return c
 
     lax.fori_loop(1, n, wait_idx, 0)
-    to_smem = pltpu.make_async_copy(asked_vmem, asked_ref, asked_sem)
+    to_smem = pltpu.make_async_copy(asked_vmem, asked_ref, out_sem.at[1])
     to_smem.start()
     to_smem.wait()
     base = me * slots % width
@@ -164,18 +209,22 @@
         p = (me + k) % n
         for s in range(slots):
             served_ref[p * slots + s] = rad_ref[asked_ref[p, 0, base + s]]
-            asked_out[0, p * slots + s] = asked_ref[p, 0, base + s]
-
-        @pl.when(k != 0)
+
+        @pl.when(k != n)
         def _():
             rad_copy(k).start()
 
         return c
 
-    lax.fori_loop(0, n, serve, 0)
-    own = pl.ds(me * slots, slots)
-    fetched_ref[own] = served_ref[own]
-    arrived_ref[own] = bwd_ref[own]
+    lax.fori_loop(1, n + 1, serve, 0)
+    for s in range(slots):
+        fetched_ref[me * slots + s] = served_ref[me * slots + s]
+    keep_asked = pltpu.make_async_copy(asked_vmem, asked_hbm, out_sem.at[1])
+    keep_asked.start()
+
+    def fwd_copy(k):
+        mine = pl.ds((me + n - k) % n * slots, slots)
+        return pltpu.make_async_copy(fwd_ref.at[mine], fwd_hbm.at[mine], out_sem.at[2])
 
     def forward(t, c):
         for u in range(GROUP):
@@ -194,6 +243,8 @@
                     fetched_ref[l], form, (((1,), (1,)), ((), ())), preferred_element_type=F32
                 )
                 fwd_ref[l] = got * live_of(p, s)
+        for u in range(GROUP):
+            fwd_copy(t * GROUP + u).start()
         return c
 
     lax.fori_loop(0, n // GROUP, forward, 0)
@@ -208,13 +259,53 @@
         pltpu.make_async_copy(buf.at[most], buf.at[most], send_sems.at[which]).wait()
     rows = asked_vmem.at[pl.ds(0, n - 1)]
     pltpu.make_async_copy(rows, rows, send_sems.at[0]).wait()
+    keep_own.wait()
+    keep_asked.wait()
+    pltpu.make_async_copy(fwd_ref, fwd_hbm, out_sem.at[2]).wait()
 
 
 def combine(
-    target_ref, asked_ref, fwd_ref, arrived_ref, em_ref, refl_ref, area_ref, out_ref, gath, ret
+    n,
+    inner,
+    target_hbm,
+    asked_hbm,
+    fwd_hbm,
+    arrived_hbm,
+    em_ref,
+    refl_ref,
+    area_ref,
+    out_hbm,
+    target_ref,
+    asked_ref,
+    fwd_ref,
+    arrived_ref,
+    gath,
+    ret,
+    out_ref,
+    in_sem,
+    out_sem,
 ):
+    me = lax.axis_index("gx") * inner + lax.axis_index("gy")
     clusters = em_ref.shape[0]
     links = fwd_ref.shape[0]
+    slots = links // n
+    width = asked_ref.shape[2]
+    base = me * slots % width
+    parts = out_sem.shape[0]
+    step = clusters // parts
+    loads = [
+        pltpu.make_async_copy(src, dst, in_sem.at[i])
+        for i, (src, dst) in enumerate(
+            (
+                (fwd_hbm, fwd_ref),
+                (arrived_hbm, arrived_ref),
+                (target_hbm, target_ref),
+                (asked_hbm, asked_ref),
+            )
+        )
+    ]
+    for load in loads:
+        load.start()
 
     def clear(c, carry):
         gath[c] = jnp.zeros(gath.shape[1:], F32)
@@ -222,22 +313,33 @@
         return carry
 
     lax.fori_loop(0, clusters, clear, 0, unroll=8)
-
-    def scatter(l, carry):
-        t = target_ref[0, l]
-        s = asked_ref[0, l]
-        gath[t] += fwd_ref[l]
-        ret[s] += arrived_ref[l].astype(F32)
+    for load in loads:
+        load.wait()
+
+    def scatter(p, carry):
+        for s in range(slots):
+            l = p * slots + s
+            t = target_ref[0, l]
+            c = asked_ref[p, 0, base + s]
+            gath[t] += fwd_ref[l]
+            ret[c] += arrived_ref[l].astype(F32)
         return carry
 
-    lax.fori_loop(0, links, scatter, 0, unroll=8)
+    lax.fori_loop(0, n, scatter, 0, unroll=2)
 
     def finish(c, carry):
         area = area_ref[pl.ds(c, 1), :]
         out_ref[c] = em_ref[c] + refl_ref[c] * (gath[c] + ret[c] / area)
         return carry
 
-    lax.fori_loop(0, clusters, finish, 0, unroll=8)
+    stores = []
+    for i in range(parts):
+        lax.fori_loop(i * step, (i + 1) * step, finish, 0, unroll=8)
+        rows = pl.ds(i * step, step)
+        stores.append(pltpu.make_async_copy(out_ref.at[rows], out_hbm.at[rows], out_sem.at[i]))
+        stores[-1].start()
+    for store in stores:
+        store.wait()
 
 
 def solution(mesh):
@@ -260,7 +362,6 @@
         slots = links // n
         tile = (bands, patches)
         vm = pl.BlockSpec(memory_space=pltpu.VMEM)
-        sm = pl.BlockSpec(memory_space=pltpu.SMEM)
         hbm = pl.BlockSpec(memory_space=pl.ANY)
         width = min(links, LANES)
         parts = 4
@@ -269,27 +370,35 @@
             out_shape=(
                 jax.ShapeDtypeStruct((links,) + tile, F32),
                 jax.ShapeDtypeStruct((links,) + tile, BF16),
-                jax.ShapeDtypeStruct((1, links), jnp.int32),
+                jax.ShapeDtypeStruct((n, 1, width), jnp.int32),
             ),
-            in_specs=[sm, sm, sm, vm, vm, vm, hbm],
-            out_specs=(vm, vm, sm),
+            in_specs=[hbm] * 7,
+            out_specs=(hbm, hbm, hbm),
             scratch_shapes=[
+                pltpu.SMEM(block_index.shape, jnp.int32),
+                pltpu.SMEM(target_index.shape, jnp.int32),
+                pltpu.SMEM(valid_count.shape, jnp.int32),
+                pltpu.VMEM(source_index.shape, jnp.int32),
+                pltpu.VMEM(radiance.shape, BF16),
+                pltpu.VMEM(patch_area.shape, F32),
                 pltpu.VMEM(form_factor.shape, BF16),
                 pltpu.VMEM((clusters,) + tile, BF16),
                 pltpu.VMEM((links,) + tile, BF16),
                 pltpu.VMEM((links,) + tile, BF16),
                 pltpu.VMEM((links,) + tile, BF16),
+                pltpu.VMEM((links,) + tile, F32),
                 pltpu.VMEM((n, 1, width), jnp.int32),
                 pltpu.SMEM((n, 1, width), jnp.int32),
                 pltpu.SemaphoreType.DMA((parts,)),
-                pltpu.SemaphoreType.DMA,
+                pltpu.SemaphoreType.DMA((6,)),
+                pltpu.SemaphoreType.DMA((3,)),
                 pltpu.SemaphoreType.DMA((3,)),
                 pltpu.SemaphoreType.DMA((n,)),
                 pltpu.SemaphoreType.DMA((n,)),
                 pltpu.SemaphoreType.DMA((n,)),
             ],
             compiler_params=pltpu.CompilerParams(
-                collective_id=0, has_side_effects=True, vmem_limit_bytes=60 * 1024 * 1024
+                collective_id=0, has_side_effects=True, vmem_limit_bytes=EXCHANGE_MIB * 1024 * 1024
             ),
             name="exchange",
         )(
@@ -302,12 +411,22 @@
             form_factor,
         )
         return pl.pallas_call(
-            combine,
+            functools.partial(combine, n, inner),
             out_shape=jax.ShapeDtypeStruct((clusters,) + tile, F32),
-            in_specs=[sm, sm, vm, vm, vm, vm, vm],
-            out_specs=vm,
-            scratch_shapes=[pltpu.VMEM((clusters,) + tile, F32)] * 2,
-            compiler_params=pltpu.CompilerParams(vmem_limit_bytes=24 * 1024 * 1024),
+            in_specs=[hbm, hbm, hbm, hbm, vm, vm, vm],
+            out_specs=hbm,
+            scratch_shapes=[
+                pltpu.SMEM(target_index.shape, jnp.int32),
+                pltpu.SMEM((n, 1, width), jnp.int32),
+                pltpu.VMEM((links,) + tile, F32),
+                pltpu.VMEM((links,) + tile, BF16),
+                pltpu.VMEM((clusters,) + tile, F32),
+                pltpu.VMEM((clusters,) + tile, F32),
+                pltpu.VMEM((clusters,) + tile, F32),
+                pltpu.SemaphoreType.DMA((4,)),
+                pltpu.SemaphoreType.DMA((4,)),
+            ],
+            compiler_params=pltpu.CompilerParams(vmem_limit_bytes=COMBINE_MIB * 1024 * 1024),
             name="combine",
         )(target_index, asked, fwd, arrived, emission, reflectance, patch_area)
 

time: 39.5 us -> 37.1 us (0.939)
  the two profiles are of different devices: /device:TPU:29 before, /device:TPU:0 now
where the time goes in v2:
time: 37.1 us; the launch traced here: 37 us
  Pallas kernels  36.9 us (99%)
    pallas_call x1, Pallas kernels, shards(): pl.pallas_call(functools.partial(exchange, n, inner), out_shape=(jax.Shap...  32.8 us
    pallas_call x1, Pallas kernels, shards(): pl.pallas_call(functools.partial(combine, n, inner), out_shape=jax.ShapeD...  4.11 us

profile of v2, /device:TPU:0, one launch (start us, length us, event | category | flops | bytes accessed | tf_op | source)
XLA Modules:
  0.0 37.0 jit_solution(1395559464295727638)
XLA Ops:
  0.0 32.8 %exchange.1 = (f32[128,16,128]{2,1,0:T(8,128)}, bf16[128,16,128]{2,1,0:T(8,128)(2,1)}, s32[32,1,128]{2,1,0:T(1,128)}) custom-call(s32[1,128]{1,0:T(1,128)} %block_hbm.1, s32[1,128]{1,0:T(1,128)} %target_hbm.3, s32[1,32]{1,0:T(1,128)} %count_hbm.1, s32[1,128]{1,0:T(1,128)} %source_hbm.1, bf16[64,16,128]{2,1,0:T(8,128)(2,1)} %rad_hbm.1, f32[64,128]{1,0:T(8,128)} %area_ref.1, ...), custom_call_target="tpu_custom_call" | custom-call | tf_op jit(solution)/shard_map/exchange/pallas_call | solution.py:368
  32.8 4.1 %combine.1 = f32[64,16,128]{2,1,0:T(8,128)} custom-call(s32[1,128]{1,0:T(1,128)} %target_hbm.3, s32[32,1,128]{2,1,0:T(1,128)} %get-tuple-element.8.asked_hbm, f32[128,16,128]{2,1,0:T(8,128)} %get-tuple-element.9.fwd_hbm, bf16[128,16,128]{2,1,0:T(8,128)(2,1)} %get-tuple-element.10.arrived_hbm, f32[64,16,128]{2,1,0:T(8,128)} %em_ref.1, ...), custom_call_target="tpu_custom_call" | custom-call | tf_op jit(solution)/shard_map/combine/pallas_call | solution.py:413

commit v3 on v2

--- a/solution.py
+++ b/solution.py
@@ -271,10 +271,13 @@
     asked_hbm,
     fwd_hbm,
     arrived_hbm,
+    em_hbm,
+    refl_hbm,
+    area_hbm,
+    out_hbm,
     em_ref,
     refl_ref,
     area_ref,
-    out_hbm,
     target_ref,
     asked_ref,
     fwd_ref,
@@ -301,6 +304,9 @@
                 (arrived_hbm, arrived_ref),
                 (target_hbm, target_ref),
                 (asked_hbm, asked_ref),
+                (em_hbm, em_ref),
+                (refl_hbm, refl_ref),
+                (area_hbm, area_ref),
             )
         )
     ]
@@ -313,7 +319,7 @@
         return carry
 
     lax.fori_loop(0, clusters, clear, 0, unroll=8)
-    for load in loads:
+    for load in loads[:4]:
         load.wait()
 
     def scatter(p, carry):
@@ -332,6 +338,8 @@
         out_ref[c] = em_ref[c] + refl_ref[c] * (gath[c] + ret[c] / area)
         return carry
 
+    for load in loads[4:]:
+        load.wait()
     stores = []
     for i in range(parts):
         lax.fori_loop(i * step, (i + 1) * step, finish, 0, unroll=8)
@@ -361,7 +369,6 @@
         links = source_index.shape[1]
         slots = links // n
         tile = (bands, patches)
-        vm = pl.BlockSpec(memory_space=pltpu.VMEM)
         hbm = pl.BlockSpec(memory_space=pl.ANY)
         width = min(links, LANES)
         parts = 4
@@ -413,9 +420,12 @@
         return pl.pallas_call(
             functools.partial(combine, n, inner),
             out_shape=jax.ShapeDtypeStruct((clusters,) + tile, F32),
-            in_specs=[hbm, hbm, hbm, hbm, vm, vm, vm],
+            in_specs=[hbm] * 7,
             out_specs=hbm,
             scratch_shapes=[
+                pltpu.VMEM((clusters,) + tile, F32),
+                pltpu.VMEM((clusters,) + tile, F32),
+                pltpu.VMEM(patch_area.shape, F32),
                 pltpu.SMEM(target_index.shape, jnp.int32),
                 pltpu.SMEM((n, 1, width), jnp.int32),
                 pltpu.VMEM((links,) + tile, F32),
@@ -423,7 +433,7 @@
                 pltpu.VMEM((clusters,) + tile, F32),
                 pltpu.VMEM((clusters,) + tile, F32),
                 pltpu.VMEM((clusters,) + tile, F32),
-                pltpu.SemaphoreType.DMA((4,)),
+                pltpu.SemaphoreType.DMA((7,)),
                 pltpu.SemaphoreType.DMA((4,)),
             ],
             compiler_params=pltpu.CompilerParams(vmem_limit_bytes=COMBINE_MIB * 1024 * 1024),

time: 37.1 us -> 35.9 us (0.968)
  Pallas kernels: 36.9 us -> 35.8 us
    pallas_call x1, Pallas kernels: 4.11 us -> 2.93 us  [shards(): pl.pallas_call(functools.partial(combine, n, inner), out_shape=jax.ShapeD...]
where the time goes in v3:
time: 35.9 us; the launch traced here: 35.8 us
  Pallas kernels  35.8 us (100%)
    pallas_call x1, Pallas kernels, shards(): pl.pallas_call(functools.partial(exchange, n, inner), out_shape=(jax.Shap...  32.8 us
    pallas_call x1, Pallas kernels, shards(): pl.pallas_call(functools.partial(combine, n, inner), out_shape=jax.ShapeD...  2.93 us

profile of v3, /device:TPU:0, one launch (start us, length us, event | category | flops | bytes accessed | tf_op | source)
XLA Modules:
  0.0 35.8 jit_solution(16836066432851325502)
XLA Ops:
  0.0 32.8 %exchange.1 = (f32[128,16,128]{2,1,0:T(8,128)}, bf16[128,16,128]{2,1,0:T(8,128)(2,1)}, s32[32,1,128]{2,1,0:T(1,128)}) custom-call(s32[1,128]{1,0:T(1,128)} %block_hbm.1, s32[1,128]{1,0:T(1,128)} %target_hbm.3, s32[1,32]{1,0:T(1,128)} %count_hbm.1, s32[1,128]{1,0:T(1,128)} %source_hbm.1, bf16[64,16,128]{2,1,0:T(8,128)(2,1)} %rad_hbm.1, f32[64,128]{1,0:T(8,128)} %area_hbm.3, ...), custom_call_target="tpu_custom_call" | custom-call | tf_op jit(solution)/shard_map/exchange/pallas_call | solution.py:375
  32.9 2.9 %combine.1 = f32[64,16,128]{2,1,0:T(8,128)} custom-call(s32[1,128]{1,0:T(1,128)} %target_hbm.3, s32[32,1,128]{2,1,0:T(1,128)} %get-tuple-element.8.asked_hbm, f32[128,16,128]{2,1,0:T(8,128)} %get-tuple-element.9.fwd_hbm, bf16[128,16,128]{2,1,0:T(8,128)(2,1)} %get-tuple-element.10.arrived_hbm, f32[64,16,128]{2,1,0:T(8,128)} %em_hbm.1, ...), custom_call_target="tpu_custom_call" | custom-call | tf_op jit(solution)/shard_map/combine/pallas_call | solution.py:420
